TPU v7x, 32 devices: a whole 2x2x4 slice. The times are simulated.
32 devices in a mesh: groups: 2 (over y), row: 4 (over z), head: 4 (over x, core).
Axes of the slice: x: 2, y: 2, z: 4, core: 2. Of those that a mesh axis runs over, the one named last changes fastest.
Arguments:
- tokens: bfloat16 [32, 2048], P('groups'), parts along dimension 0, may hold values from -6 to 6
- query_weight: bfloat16 [2048, 3072], P('row', 'head'), may hold values from -0.125 to 0.125
- latent_weight: bfloat16 [512, 4096], P('row', 'head'), may hold values from -0.25 to 0.25
- output_weight: bfloat16 [2048, 2048], P('row', 'head'), may hold values from -0.5 to 0.5
- cache_latent: bfloat16 [32, 2048, 512], P(('groups', 'row'), 'head'), parts along dimension 0, may hold values from -32 to 32
- cache_rope: bfloat16 [32, 64, 2048], P(('groups', 'row'), None, 'head'), parts along dimension 0, may hold values from -1800 to 1800
- lengths: int32 [32], P('groups'), parts along dimension 0, may hold values from 1 to 2048
- slot_seq: int32 [32], P('groups'), parts along dimension 0, may hold values from 0 to 15, each once
Outputs:
- attn_out: bfloat16 [32, 2048], P(('groups', 'row'), 'head'), parts along dimension 0
There are 2 independent parts, one for each index of `groups`. A program takes and returns all parts, laid end to end along the dimension named above; an argument that names none is the same for every part. Nothing has to cross between parts.
Inputs may be any that keep to these rules, and one draw needn't show every extreme that they name: Cache row i belongs to sequence slot_seq[i], and output row i is that sequence's. Positions at or past lengths[s] of a sequence hold stale entries that are not read; its new token stands at position lengths[s] - 1.
All inputs are finite; a program needn't handle non-finite values.
Results may differ from a plain program's by a relative error of at most 0.039.
Values may be sent and summed in bfloat16 or wider, within the bound.
A program may use at most 64 MiB of HBM per device.

v0:
```python
import jax
import jax.numpy as jnp
from jax import lax
from jax.sharding import PartitionSpec as P

D = 2048
H = 16
NOPE = 128
ROPE = 64
V = 128
LAT = 512
BLOCK = 256
neg_big = -1e30


def combined_all(part, axis, combine):
    gathered = jax.tree.map(lambda a: lax.all_gather(a, axis), part)

    def take(source):
        return jax.tree.map(lambda a: lax.dynamic_index_in_dim(a, source, 0, False), gathered)

    return lax.fori_loop(
        1, lax.axis_size(axis), lambda source, state: combine(state, take(source)), take(0)
    )


def absorb(query_weight, output_weight, kv_heads):
    width = query_weight.shape[0]
    head_total = kv_heads.shape[1]
    query_heads = query_weight.reshape(width, head_total, NOPE + ROPE)
    out_heads = output_weight.reshape(width, head_total, V)
    nope_part = jnp.einsum(
        "dhn,lhn->dhl",
        query_heads[:, :, :NOPE],
        kv_heads[:, :, :NOPE],
        preferred_element_type=jnp.float32,
    ).astype(jnp.bfloat16)
    query_abs = jnp.concatenate([nope_part, query_heads[:, :, NOPE:]], axis=2).reshape(width, -1)
    out_abs = jnp.einsum(
        "dhv,lhv->dhl", out_heads, kv_heads[:, :, NOPE:], preferred_element_type=jnp.float32
    ).astype(jnp.bfloat16)
    return (query_abs, out_abs.reshape(width, -1))


def rotate(queries, seq_len):
    half_width = ROPE // 2
    inverse_freq = jnp.power(10000.0, -2.0 * jnp.arange(half_width, dtype=jnp.float32) / ROPE)
    angles = (seq_len - 1).astype(jnp.float32)[:, None] * inverse_freq[None, :]
    cosine = jnp.cos(angles)[:, None, :]
    sine = jnp.sin(angles)[:, None, :]
    first_half = queries[:, :, LAT : LAT + half_width]
    second_half = queries[:, :, LAT + half_width :]
    rotated = jnp.concatenate(
        [first_half * cosine - second_half * sine, first_half * sine + second_half * cosine], axis=2
    )
    return jnp.concatenate([queries[:, :, :LAT], rotated], axis=2)


def combine(earlier, later):
    earlier_max, earlier_sum, earlier_acc = earlier
    later_max, later_sum, later_acc = later
    peak_max = jnp.maximum(earlier_max, later_max)
    earlier_scale = jnp.exp(earlier_max - peak_max)
    later_scale = jnp.exp(later_max - peak_max)
    summed = earlier_sum * earlier_scale + later_sum * later_scale
    weighted = earlier_acc * earlier_scale[..., None] + later_acc * later_scale[..., None]
    return (peak_max, summed, weighted)


def local(
    tokens, query_weight, latent_weight, output_weight, cache_latent, cache_rope, lengths, slot_seq
):
    heads_dev = query_weight.shape[1] // (NOPE + ROPE)
    seq_dev = cache_latent.shape[0]
    seg_len = cache_latent.shape[1]
    latent_full = lax.all_gather(latent_weight, "row", axis=0, tiled=True)
    kv_heads = latent_full.reshape(LAT, heads_dev, NOPE + V)
    full_query, full_out = (
        lax.all_gather(query_weight, "row", axis=0, tiled=True),
        lax.all_gather(output_weight, "row", axis=0, tiled=True),
    )
    query_abs, out_abs = absorb(full_query, full_out, kv_heads)
    first_row = lax.axis_index("row") * seq_dev
    seq_ids = lax.dynamic_slice_in_dim(slot_seq, first_row, seq_dev)
    chosen = tokens[seq_ids]
    seq_len = lengths[seq_ids]
    queries = jnp.dot(chosen, query_abs, preferred_element_type=jnp.float32).reshape(
        seq_dev, heads_dev, LAT + ROPE
    )
    queries = (
        rotate(queries, seq_len).astype(jnp.bfloat16).reshape(seq_dev, heads_dev * (LAT + ROPE))
    )
    queries = lax.all_gather(queries, "head", axis=1, tiled=True).reshape(seq_dev, H, LAT + ROPE)
    query_latent = queries[:, :, :LAT]
    query_rope = queries[:, :, LAT:]
    score_scale = 1.0 / jnp.sqrt(jnp.float32(NOPE + ROPE))
    offset = lax.axis_index("head") * seg_len
    local_len = jnp.clip(seq_len - offset, 0, seg_len)
    live_blocks = (jnp.max(local_len) + BLOCK - 1) // BLOCK

    def advance(block_idx, running):
        run_max, run_sum, run_acc = running
        begin_at = block_idx * BLOCK
        latent_blk = lax.dynamic_slice_in_dim(cache_latent, begin_at, BLOCK, 1)
        rope_blk = lax.dynamic_slice_in_dim(cache_rope, begin_at, BLOCK, 2)
        scores = jnp.einsum(
            "bhl,btl->bht", query_latent, latent_blk, preferred_element_type=jnp.float32
        )
        scores = (
            scores
            + jnp.einsum("bhr,brt->bht", query_rope, rope_blk, preferred_element_type=jnp.float32)
        ) * score_scale
        in_range = (begin_at + jnp.arange(BLOCK, dtype=jnp.int32))[None, None, :] < local_len[
            :, None, None
        ]
        masked = jnp.where(in_range, scores, neg_big)
        new_max = jnp.maximum(run_max, jnp.max(masked, axis=2))
        weights = jnp.where(in_range, jnp.exp(masked - new_max[..., None]), 0.0)
        factor = jnp.exp(run_max - new_max)
        run_sum = run_sum * factor + jnp.sum(weights, axis=2)
        run_acc = run_acc * factor[..., None] + jnp.einsum(
            "bht,btl->bhl",
            weights.astype(jnp.bfloat16),
            latent_blk,
            preferred_element_type=jnp.float32,
        )
        return (new_max, run_sum, run_acc)

    initial = (
        jnp.full((seq_dev, H), neg_big, jnp.float32),
        jnp.zeros((seq_dev, H), jnp.float32),
        jnp.zeros((seq_dev, H, LAT), jnp.float32),
    )
    partial_state = lax.fori_loop(0, live_blocks, advance, initial)
    merged_max, merged_sum, merged_acc = combined_all(partial_state, "head", combine)
    latent_out = (merged_acc / merged_sum[..., None]).astype(jnp.bfloat16)
    own_heads = lax.dynamic_slice_in_dim(
        latent_out, lax.axis_index("head") * heads_dev, heads_dev, 1
    )
    out_term = jnp.einsum(
        "bhl,dhl->bd",
        own_heads,
        out_abs.reshape(D, heads_dev, LAT),
        preferred_element_type=jnp.float32,
    )
    return lax.psum_scatter(out_term, "head", scatter_dimension=1, tiled=True).astype(jnp.bfloat16)


def solution(mesh):
    placed = (
        P("groups", None),
        P("row", "head"),
        P("row", "head"),
        P("row", "head"),
        P(("groups", "row"), "head", None),
        P(("groups", "row"), None, "head"),
        P("groups"),
        P("groups"),
    )
    return jax.shard_map(
        local, mesh=mesh, in_specs=placed, out_specs=P(("groups", "row"), "head"), check_vma=False
    )
```

profile of v0, /device:TPU:0, one launch (start us, length us, event | category | flops | bytes accessed | tf_op | source)
XLA Modules:
  0.0 190.2 jit_solution(7725425204575464518)
XLA Ops:
  6.5 2.3 %copy.30 = bf16[512,768]{0,1:T(8,128)(2,1)} copy(bf16[512,768]{1,0:T(8,128)(2,1)} %param.13) | data formatting | bytes 1572864 | tf_op args[1]
  9.0 1.8 copy.28
  10.8 2.0 %copy.36 = bf16[512,512]{0,1:T(8,128)(2,1)} copy(bf16[512,512]{1,0:T(8,128)(2,1)} %param.15) | data formatting | bytes 1048576 | tf_op args[3]
  13.0 0.7 compare_select_fusion
  13.7 1.3 gather_fusion
  15.0 0.6 fusion.42
  16.3 0.6 gather_fusion.1
  16.9 0.1 multiply_cosine_fusion
  17.0 58.2 %all-gather.11.cloned.1.call-done = bf16[2048,768]{0,1:T(8,128)(2,1)} async-done(((bf16[512,768]{0,1:T(8,128)(2,1)}), bf16[2048,768]{0,1:T(8,128)(2,1)}) %all-gather.11.cloned.1.call-update) | async-done | bytes 3145744 | tf_op jit(solution)/shard_map/all_gather | solution.py:79
  75.2 2.3 %slice.51 = bf16[2048,4,64]{0,2,1:T(8,128)(2,1)} slice(bf16[2048,4,192]{0,2,1:T(8,128)(2,1)} %bitcast.61), slice={[0:2048], [0:4], [128:192]} | slice | bytes 2097152 | tf_op jit(solution)/shard_map/slice | solution.py:38
  77.5 27.8 %all-gather.9.cloned.1.call-done = bf16[512,1024]{0,1:T(8,128)(2,1)} async-done(((bf16[128,1024]{0,1:T(8,128)(2,1)}), bf16[512,1024]{0,1:T(8,128)(2,1)}) %all-gather.9.cloned.1.call-update) | async-done | bytes 1048592 | tf_op jit(solution)/shard_map/all_gather | solution.py:76
  105.4 4.2 %convert_bitcast_fusion = bf16[2048,4,512]{0,2,1:T(8,128)(2,1)S(1)} fusion(bf16[2048,4,192]{0,2,1:T(8,128)(2,1)} %bitcast.62, bf16[512,4,256]{0,2,1:T(8,128)(2,1)} %bitcast.64), kind=kOutput, calls=%fused_computation.40 | convolution fusion | flops 1077936128 | bytes 11010048 | tf_op jit(solution)/shard_map/dhn,lhn->dhl/dot_general | solution.py:32
  109.6 2.8 %fusion.20 = f32[4,4,576]{2,0,1:T(4,128)S(1)} fusion(bf16[2048,4,64]{0,2,1:T(8,128)(2,1)S(1)} %copy-done.3, bf16[2048,4,512]{0,2,1:T(8,128)(2,1)S(1)} %convert_bitcast_fusion, bf16[4,2048]{1,0:T(4,128)(2,1)S(1)} %gather_fusion.1), kind=kOutput, calls=%fused_computation.34 | convolution fusion | flops 56623104 | bytes 9490432 | tf_op jit(solution)/shard_map/dot_general | solution.py:87
  112.7 5.3 %all_gather.32 = bf16[4,9216]{1,0:T(4,128)(2,1)S(1)} all-gather(bf16[4,2304]{1,0:T(4,128)(2,1)S(1)} %convert_element_type.36), channel_id=1, replica_groups=mesh['groups'=2,'row'=4,'head'=4] {'head'}, dimensions={1}, use_global_device_ids=true | all-gather | bytes 92160 | tf_op jit(solution)/shard_map/all_gather | solution.py:93
  118.0 0.1 reshape.117
  118.2 2.4 %while.33 = (s32[]{:T(128)}, f32[4,16]{1,0:T(4,128)S(1)}, f32[4,16]{1,0:T(4,128)S(1)}, f32[4,16,512]{2,1,0:T(8,128)S(1)}, s32[]{:T(128)}, /*index=5*/s32[4]{0:T(...) while((s32[]{:T(128)}, f32[4,16]{1,0:T(4,128)S(1)}, ...), condition=%wide.region_4.5_spmd, body=%wide.region_1.4_spmd.sunk | while | flops 35882372 | bytes 2914003 | solution.py:134
  118.2 0.4 fusion.62
  118.7 0.2 fusion.63
  119.0 0.2 fusion.64
  119.1 0.3 convolution_add_fusion.3
  119.5 0.4 fusion.62
  119.9 0.2 fusion.63
  120.2 0.2 fusion.64
  120.3 0.3 convolution_add_fusion.3
  120.6 7.3 %all-gather.2 = f32[16,16,512]{2,1,0:T(8,128)S(1)} all-gather(f32[4,16,512]{2,1,0:T(8,128)S(1)} %get-tuple-element.239), channel_id=4, replica_groups=mesh['groups'=2,'row'=4,'head'=4] {'head'}, dimensions={0}, use_global_device_ids=true | all-gather | bytes 655360 | tf_op jit(solution)/shard_map/all_gather | solution.py:17
  127.9 5.2 %all-gather.4 = f32[4,4,16]{2,1,0:T(4,128)S(1)} all-gather(f32[1,4,16]{2,1,0:T(4,128)S(1)} %bitcast.68), channel_id=3, replica_groups=mesh['groups'=2,'row'=4,'head'=4] {'head'}, dimensions={0}, use_global_device_ids=true | all-gather | bytes 1280 | tf_op jit(solution)/shard_map/all_gather | solution.py:17
  133.1 5.2 %all-gather.3 = f32[4,4,16]{2,1,0:T(4,128)S(1)} all-gather(f32[1,4,16]{2,1,0:T(4,128)S(1)} %bitcast.66), channel_id=2, replica_groups=mesh['groups'=2,'row'=4,'head'=4] {'head'}, dimensions={0}, use_global_device_ids=true | all-gather | bytes 1280 | tf_op jit(solution)/shard_map/all_gather | solution.py:17
  138.3 0.4 while.34
  138.9 12.0 %all-gather.13.cloned.1.call-done = bf16[2048,512]{0,1:T(8,128)(2,1)} async-done(((bf16[512,512]{0,1:T(8,128)(2,1)}), bf16[2048,512]{0,1:T(8,128)(2,1)}) %all-gather.13.cloned.1.call-update) | async-done | bytes 2097168 | tf_op jit(solution)/shard_map/all_gather | solution.py:80
  151.0 7.3 %fusion.28 = f32[2048,4]{1,0:T(8,128)} fusion(bf16[2048,4,128]{0,2,1:T(8,128)(2,1)} %bitcast.69, bf16[512,4,256]{0,2,1:T(8,128)(2,1)} %bitcast.65, f32[4,16,512]{2,0,1:T(4,128)S(1)} %copy.34, s32[]{:T(128)S(6)} %select_n.49, f32[4,4]{0,1:T(4,128)S(1)} %constant_dynamic-slice_fusion), kind=kOutput, calls=%fused_computation.42 | convolution fusion | flops 1111506944 | bytes 2689028 | tf_op jit(solution)/shard_map/bhl,dhl->bd/dot_general | solution.py:140
  158.3 23.7 %reduce-scatter.4.cloned.1.call-done = f32[512,4]{1,0:T(8,128)} async-done(((f32[2048,4]{1,0:T(8,128)}), f32[512,4]{1,0:T(8,128)}) %reduce-scatter.4.cloned.1.call-update) | async-done | bytes 8208
  182.0 1.7 copy.42
  (50 shorter events, 1.3 us)
Async XLA Ops:
  6.5 9.8 %copy-start = (bf16[16,2048]{1,0:T(8,128)(2,1)S(1)}, bf16[16,2048]{1,0:T(8,128)(2,1)}, u32[]{:S(2)}) copy-start(bf16[16,2048]{1,0:T(8,128)(2,1)} %param.12) | copy-start | bytes 196612
  6.5 68.7 %all-gather.11.cloned.1.call-start = ((), (), s32[]{:S(2)}) async-start(), calls=%async_computation.2 | async-start | bytes 3932160 | tf_op jit(solution)/shard_map/all_gather | solution.py:79
  8.9 96.5 %all-gather.9.cloned.1.call-start = ((), (), s32[]{:S(2)}) async-start(), calls=%async_computation.1 | async-start | bytes 1310720 | tf_op jit(solution)/shard_map/all_gather | solution.py:76
  10.8 140.2 %all-gather.13.cloned.1.call-start = ((), (), s32[]{:S(2)}) async-start(), calls=%async_computation.3 | async-start | bytes 2621440 | tf_op jit(solution)/shard_map/all_gather | solution.py:80
  12.9 169.1 %reduce-scatter.4.cloned.1.call-start = ((), (), s32[]{:S(2)}) async-start(), calls=%async_computation.4 | async-start | bytes 1310720
  105.4 4.2 %copy-start.3 = (bf16[2048,4,64]{0,2,1:T(8,128)(2,1)S(1)}, bf16[2048,4,64]{0,2,1:T(8,128)(2,1)}, u32[]{:S(2)}) copy-start(bf16[2048,4,64]{0,2,1:T(8,128)(2,1)} %slice.51) | copy-start | bytes 3145732
  109.6 8.6 %copy-start.1 = (bf16[4,512,512]{2,1,0:T(8,128)(2,1)S(1)}, bf16[4,512,512]{2,1,0:T(8,128)(2,1)}, u32[]{:S(2)}) copy-start(bf16[4,512,512]{2,1,0:T(8,128)(2,1)} %param.16) | copy-start | bytes 6291460
  109.6 8.6 %copy-start.2 = (bf16[4,64,512]{2,1,0:T(8,128)(2,1)S(1)}, bf16[4,64,512]{2,1,0:T(8,128)(2,1)}, u32[]{:S(2)}) copy-start(bf16[4,64,512]{2,1,0:T(8,128)(2,1)} %param.17) | copy-start | bytes 786436
Sparse Core Ops, SparseCore 0:
  9.0 66.1 all-gather.10
  76.8 28.5 all-gather.8
  107.0 43.9 all-gather.12
  158.4 23.5 reduce-scatter.3
where the time goes:
time: 191 us; the launch traced here: 190 us
  waiting for transfers between devices  122 us (64%)
  blocking collectives  22.9 us (12%)
  matrix products  16.1 us (8%)
  between operations  14 us (7%)
  local copies, waits for them, and re-layouts  12.5 us (7%)
  other arithmetic  2.54 us (1%)
    all_gather x1, waiting for transfers between devices, local(): lax.all_gather(query_weight, 'row', axis=0, tiled=True)  58.2 us
    all_gather x1, waiting for transfers between devices, local(): latent_full = lax.all_gather(latent_weight, 'row', axis=0, tiled=True)  27.8 us
    unnamed x5, waiting for transfers between devices  23.8 us
    all_gather x3, blocking collectives, combined_all(): gathered = jax.tree.map(lambda a: lax.all_gather(a, axis), part)  17.6 us
    all_gather x1, waiting for transfers between devices, local(): lax.all_gather(output_weight, 'row', axis=0, tiled=True)  12 us
    unnamed x12, local copies, waits for them, and re-layouts  7.88 us
    dot_general x1, matrix products, local(): jnp.einsum('bhl,dhl->bd', own_heads, out_abs.reshape(D, heads_dev, LAT),...  7.3 us
    all_gather x1, blocking collectives, local(): lax.all_gather(queries, 'head', axis=1, tiled=True)  5.26 us
  transfers between devices with their start and end apart: 4, of which 4 were waited for; matrix products, arithmetic and copies ran while one was open for 10% of the time, Pallas kernels for 0%

commit v1 on v0

--- a/solution.py
+++ b/solution.py
@@ -73,7 +73,15 @@
     heads_dev = query_weight.shape[1] // (NOPE + ROPE)
     seq_dev = cache_latent.shape[0]
     seg_len = cache_latent.shape[1]
-    latent_full = lax.all_gather(latent_weight, "row", axis=0, tiled=True)
+    axis_len = lax.axis_size("row")
+    pages = [latent_weight]
+    for dev_i in [*range(axis_len - 1)]:
+        inter = lax.ppermute(
+            pages[-1], "row", [(dd, (dd + 1) % axis_len) for dd in range(axis_len)]
+        )
+        pages.append(inter)
+    answer = jnp.concatenate(pages[::-1], axis=0)
+    latent_full = jnp.roll(answer, (lax.axis_index("row") + 1) * latent_weight.shape[0], axis=0)
     kv_heads = latent_full.reshape(LAT, heads_dev, NOPE + V)
     full_query, full_out = (
         lax.all_gather(query_weight, "row", axis=0, tiled=True),

time: 191 us -> 172 us (0.901)
  waiting for transfers between devices: 122 us -> 101 us
  starting transfers between devices: 0.13 us -> 4.29 us
  local copies, waits for them, and re-layouts: 12.5 us -> 9.04 us
    ppermute x0 -> x3, waiting for transfers between devices: none -> 36.6 us  [local(): lax.ppermute(pages[-1], 'row', [(dd, (dd + 1) % axis_len) for dd in range...]
    all_gather x1 -> x0, waiting for transfers between devices: 27.8 us -> none  [local(): latent_full = lax.all_gather(latent_weight, 'row', axis=0, tiled=True)]
    all_gather x1, waiting for transfers between devices: 58.2 us -> 31.6 us  [local(): lax.all_gather(query_weight, 'row', axis=0, tiled=True)]
    ppermute x0 -> x3, starting transfers between devices: none -> 4.17 us  [local(): lax.ppermute(pages[-1], 'row', [(dd, (dd + 1) % axis_len) for dd in range...]
    all_gather x1, waiting for transfers between devices: 12 us -> 9.38 us  [local(): lax.all_gather(output_weight, 'row', axis=0, tiled=True)]
    unnamed x12 -> x23, local copies, waits for them, and re-layouts: 7.88 us -> 5.86 us
    unnamed x5 -> x4, waiting for transfers between devices: 23.8 us -> 23.8 us
  transfers between devices with their start and end apart: 4 -> 6, of which waited for: 4 -> 6; matrix products, arithmetic and copies ran while one was open for 10% -> 10% of each run, Pallas kernels for 0% -> 0%
where the time goes in v1:
time: 172 us; the launch traced here: 171 us
  waiting for transfers between devices  101 us (59%)
  blocking collectives  22.9 us (13%)
  matrix products  17.5 us (10%)
  between operations  14.1 us (8%)
  local copies, waits for them, and re-layouts  9.04 us (5%)
  starting transfers between devices  4.29 us (2%)
  other arithmetic  1.89 us (1%)
    ppermute x3, waiting for transfers between devices, local(): lax.ppermute(pages[-1], 'row', [(dd, (dd + 1) % axis_len) for dd in range...  36.6 us
    all_gather x1, waiting for transfers between devices, local(): lax.all_gather(query_weight, 'row', axis=0, tiled=True)  31.6 us
    unnamed x4, waiting for transfers between devices  23.8 us
    all_gather x3, blocking collectives, combined_all(): gathered = jax.tree.map(lambda a: lax.all_gather(a, axis), part)  17.6 us
    all_gather x1, waiting for transfers between devices, local(): lax.all_gather(output_weight, 'row', axis=0, tiled=True)  9.38 us
    dot_general x1, matrix products, local(): jnp.einsum('bhl,dhl->bd', own_heads, out_abs.reshape(D, heads_dev, LAT),...  7.13 us
    unnamed x23, local copies, waits for them, and re-layouts  5.86 us
    all_gather x1, blocking collectives, local(): lax.all_gather(queries, 'head', axis=1, tiled=True)  5.26 us
  transfers between devices with their start and end apart: 6, of which 6 were waited for; matrix products, arithmetic and copies ran while one was open for 10% of the time, Pallas kernels for 0%

profile of v1, /device:TPU:0, one launch (start us, length us, event | category | flops | bytes accessed | tf_op | source)
XLA Modules:
  0.0 171.2 jit_solution(37791818982334649)
XLA Ops:
  6.6 2.4 %copy.36 = bf16[512,768]{0,1:T(8,128)(2,1)} copy(bf16[512,768]{1,0:T(8,128)(2,1)} %param.13) | data formatting | bytes 1572864 | tf_op args[1]
  9.3 3.1 %collective-permute-start = (bf16[128,1024]{0,1:T(8,128)(2,1)S(1)}, bf16[128,1024]{0,1:T(8,128)(2,1)S(1)}, u32[]{:S(2)}, u32[]{:S(2)}) collective-permute-start(bf16[128,1024]{0,1:T(8,128)(2,1)S(1)} %copy.32), channel_id=1, source_target_pairs={{0,4},{4,8},{8,12},{12,0},{1,5},{5,9},{9,13},{13,1},{2,6},{6,10},{... | collective-permute-start | bytes 786440 | tf_op jit(solution)/shard_map/ppermute | solution.py:79
  12.4 1.0 copy.42
  13.6 7.1 %collective-permute-done = bf16[128,1024]{0,1:T(8,128)(2,1)S(1)} collective-permute-done((bf16[128,1024]{0,1:T(8,128)(2,1)S(1)}, bf16[128,1024]{0,1:T(8,128)(2,1)S(1)}, u32[]{:S(2)}, u32[]{:S(2)}) %collective-permute-start) | collective-permute-done | bytes 262176 | tf_op jit(solution)/shard_map/ppermute | solution.py:79
  20.7 0.6 gather_fusion
  21.4 0.6 fusion.42
  22.0 14.7 %collective-permute-done.1 = bf16[128,1024]{0,1:T(8,128)(2,1)S(1)} collective-permute-done((bf16[128,1024]{0,1:T(8,128)(2,1)S(1)}, bf16[128,1024]{0,1:T(8,128)(2,1)S(1)}, u32[]{:S(2)}, u32[]{:S(2)}) %collective-permute-start.1) | collective-permute-done | bytes 262176 | tf_op jit(solution)/shard_map/ppermute | solution.py:79
  36.7 1.1 collective-permute-start.2
  38.4 0.6 gather_fusion.1
  39.1 14.8 %collective-permute-done.2 = bf16[128,1024]{0,1:T(8,128)(2,1)S(1)} collective-permute-done((bf16[128,1024]{0,1:T(8,128)(2,1)S(1)}, bf16[128,1024]{0,1:T(8,128)(2,1)S(1)}, u32[]{:S(2)}, u32[]{:S(2)}) %collective-permute-start.2) | collective-permute-done | bytes 262176 | tf_op jit(solution)/shard_map/ppermute | solution.py:79
  54.8 31.6 %all-gather.8.cloned.1.call-done = bf16[2048,768]{0,1:T(8,128)(2,1)} async-done(((bf16[512,768]{0,1:T(8,128)(2,1)}), bf16[2048,768]{0,1:T(8,128)(2,1)}) %all-gather.8.cloned.1.call-update) | async-done | bytes 3145744 | tf_op jit(solution)/shard_map/all_gather | solution.py:87
  86.4 1.3 slice.51
  87.7 4.0 %convert_bitcast_fusion = bf16[2048,4,512]{0,2,1:T(8,128)(2,1)S(1)} fusion(bf16[2048,4,192]{0,2,1:T(8,128)(2,1)} %bitcast.62, bf16[512,4,256]{0,2,1:T(8,128)(2,1)S(1)} %bitcast.64), kind=kOutput, calls=%fused_computation.40 | convolution fusion | flops 1077936128 | bytes 11010048 | tf_op jit(solution)/shard_map/dhn,lhn->dhl/dot_general | solution.py:32
  91.7 2.8 %fusion.20 = f32[4,4,576]{2,0,1:T(4,128)S(1)} fusion(bf16[2048,4,64]{0,2,1:T(8,128)(2,1)S(1)} %slice.51, bf16[2048,4,512]{0,2,1:T(8,128)(2,1)S(1)} %convert_bitcast_fusion, bf16[4,2048]{1,0:T(4,128)(2,1)S(1)} %gather_fusion.1), kind=kOutput, calls=%fused_computation.34 | convolution fusion | flops 56623104 | bytes 9490432 | tf_op jit(solution)/shard_map/dot_general | solution.py:95
  94.8 5.3 %all_gather.28 = bf16[4,9216]{1,0:T(4,128)(2,1)S(1)} all-gather(bf16[4,2304]{1,0:T(4,128)(2,1)S(1)} %convert_element_type.36), channel_id=1, replica_groups=mesh['groups'=2,'row'=4,'head'=4] {'head'}, dimensions={1}, use_global_device_ids=true | all-gather | bytes 92160 | tf_op jit(solution)/shard_map/all_gather | solution.py:101
  100.3 4.2 %while.33 = (s32[]{:T(128)}, f32[4,16]{1,0:T(4,128)S(1)}, f32[4,16]{1,0:T(4,128)S(1)}, f32[4,16,512]{2,1,0:T(8,128)S(1)}, s32[]{:T(128)}, /*index=5*/s32[4]{0:T(...) while((s32[]{:T(128)}, f32[4,16]{1,0:T(4,128)S(1)}, ...), condition=%wide.region_4.5_spmd, body=%wide.region_1.4_spmd.sunk | while | flops 35882372 | bytes 2905811 | solution.py:142
  100.3 0.4 fusion.62
  100.7 1.1 fusion.63
  101.9 0.2 fusion.64
  102.1 0.3 convolution_add_fusion.3
  102.4 0.4 fusion.62
  102.8 1.1 fusion.63
  104.0 0.2 fusion.64
  104.2 0.3 convolution_add_fusion.3
  104.5 7.3 %all-gather.2 = f32[16,16,512]{2,1,0:T(8,128)S(1)} all-gather(f32[4,16,512]{2,1,0:T(8,128)S(1)} %get-tuple-element.239), channel_id=4, replica_groups=mesh['groups'=2,'row'=4,'head'=4] {'head'}, dimensions={0}, use_global_device_ids=true | all-gather | bytes 655360 | tf_op jit(solution)/shard_map/all_gather | solution.py:17
  111.8 5.2 %all-gather.4 = f32[4,4,16]{2,1,0:T(4,128)S(1)} all-gather(f32[1,4,16]{2,1,0:T(4,128)S(1)} %bitcast.68), channel_id=3, replica_groups=mesh['groups'=2,'row'=4,'head'=4] {'head'}, dimensions={0}, use_global_device_ids=true | all-gather | bytes 1280 | tf_op jit(solution)/shard_map/all_gather | solution.py:17
  117.0 5.2 %all-gather.3 = f32[4,4,16]{2,1,0:T(4,128)S(1)} all-gather(f32[1,4,16]{2,1,0:T(4,128)S(1)} %bitcast.66), channel_id=2, replica_groups=mesh['groups'=2,'row'=4,'head'=4] {'head'}, dimensions={0}, use_global_device_ids=true | all-gather | bytes 1280 | tf_op jit(solution)/shard_map/all_gather | solution.py:17
  122.1 0.4 while.34
  122.8 9.4 %all-gather.10.cloned.1.call-done = bf16[2048,512]{0,1:T(8,128)(2,1)} async-done(((bf16[512,512]{0,1:T(8,128)(2,1)}), bf16[2048,512]{0,1:T(8,128)(2,1)}) %all-gather.10.cloned.1.call-update) | async-done | bytes 2097168 | tf_op jit(solution)/shard_map/all_gather | solution.py:88
  132.1 7.1 %fusion.28 = f32[2048,4]{1,0:T(8,128)} fusion(bf16[2048,4,128]{0,2,1:T(8,128)(2,1)} %bitcast.69, bf16[512,4,256]{0,2,1:T(8,128)(2,1)S(1)} %bitcast.65, f32[4,16,512]{2,0,1:T(4,128)S(1)} %copy.40, s32[]{:T(128)S(6)} %select_n.63, f32[4,4]{0,1:T(4,128)S(1)} %constant_dynamic-slice_fusion), kind=kOutput, calls=%fused_computation.42 | convolution fusion | flops 1111506944 | bytes 2689028 | tf_op jit(solution)/shard_map/bhl,dhl->bd/dot_general | solution.py:148
  139.3 23.7 %reduce-scatter.4.cloned.1.call-done = f32[512,4]{1,0:T(8,128)} async-done(((f32[2048,4]{1,0:T(8,128)}), f32[512,4]{1,0:T(8,128)}) %reduce-scatter.4.cloned.1.call-update) | async-done | bytes 8208
  163.0 1.7 copy.48
  (66 shorter events, 2.5 us)
Async XLA Ops:
  6.5 31.9 %copy-start = (bf16[16,2048]{1,0:T(8,128)(2,1)S(1)}, bf16[16,2048]{1,0:T(8,128)(2,1)}, u32[]{:S(2)}) copy-start(bf16[16,2048]{1,0:T(8,128)(2,1)} %param.12) | copy-start | bytes 196612
  6.5 2.5 %copy-start.4 = (bf16[128,1024]{1,0:T(8,128)(2,1)S(1)}, bf16[128,1024]{1,0:T(8,128)(2,1)}, u32[]{:S(2)}) copy-start(bf16[128,1024]{1,0:T(8,128)(2,1)} %param.14) | copy-start | bytes 786436
  6.5 5.8 %copy-start.3 = (bf16[512,512]{1,0:T(8,128)(2,1)S(1)}, bf16[512,512]{1,0:T(8,128)(2,1)}, u32[]{:S(2)}) copy-start(bf16[512,512]{1,0:T(8,128)(2,1)} %param.15) | copy-start | bytes 1572868
  6.5 6.9 %copy-start.5 = (s32[16]{0:T(128)S(1)}, s32[16]{0:T(128)}, u32[]{:S(2)}) copy-start(s32[16]{0:T(128)} %param.19) | copy-start | bytes 196
  6.5 14.2 %copy-start.1 = (s32[16]{0:T(128)S(1)}, s32[16]{0:T(128)}, u32[]{:S(2)}) copy-start(s32[16]{0:T(128)} %param.18) | copy-start | bytes 196
  6.5 79.9 %all-gather.8.cloned.1.call-start = ((), (), s32[]{:S(2)}) async-start(), calls=%async_computation.1 | async-start | bytes 3932160 | tf_op jit(solution)/shard_map/all_gather | solution.py:87
  9.0 123.1 %all-gather.10.cloned.1.call-start = ((), (), s32[]{:S(2)}) async-start(), calls=%async_computation.2 | async-start | bytes 2621440 | tf_op jit(solution)/shard_map/all_gather | solution.py:88
  9.3 11.4 %collective-permute-start = (bf16[128,1024]{0,1:T(8,128)(2,1)S(1)}, bf16[128,1024]{0,1:T(8,128)(2,1)S(1)}, u32[]{:S(2)}, u32[]{:S(2)}) collective-permute-start(bf16[128,1024]{0,1:T(8,128)(2,1)S(1)} %copy.32), channel_id=1, source_target_pairs={{0,4},{4,8},{8,12},{12,0},{1,5},{5,9},{9,13},{13,1},{2,6},{6,10},{... | collective-permute-start | bytes 786440 | tf_op jit(solution)/shard_map/ppermute | solution.py:79
  13.4 149.6 %reduce-scatter.4.cloned.1.call-start = ((), (), s32[]{:S(2)}) async-start(), calls=%async_computation.3 | async-start | bytes 1310720
  20.7 16.0 %collective-permute-start.1 = (bf16[128,1024]{0,1:T(8,128)(2,1)S(1)}, bf16[128,1024]{0,1:T(8,128)(2,1)S(1)}, u32[]{:S(2)}, u32[]{:S(2)}) collective-permute-start(bf16[128,1024]{0,1:T(8,128)(2,1)S(1)} %collective-permute-done), channel_id=1, source_target_pairs={{0,4},{4,8},{8,12},{12,0},{1,5},{5,9},{9,13},{13,1},{2,6},{6,10},{... | collective-permute-start | bytes 786440 | tf_op jit(solution)/shard_map/ppermute | solution.py:79
  36.7 17.3 %collective-permute-start.2 = (bf16[128,1024]{0,1:T(8,128)(2,1)S(1)}, bf16[128,1024]{0,1:T(8,128)(2,1)S(1)}, u32[]{:S(2)}, u32[]{:S(2)}) collective-permute-start(bf16[128,1024]{0,1:T(8,128)(2,1)S(1)} %collective-permute-done.1), channel_id=1, source_target_pairs={{0,4},{4,8},{8,12},{12,0},{1,5},{5,9},{9,13},{13,1},{2,6},{6,10},{... | collective-permute-start | bytes 786440 | tf_op jit(solution)/shard_map/ppermute | solution.py:79
  91.7 8.6 %copy-start.2 = (bf16[4,512,512]{2,1,0:T(8,128)(2,1)S(1)}, bf16[4,512,512]{2,1,0:T(8,128)(2,1)}, u32[]{:S(2)}) copy-start(bf16[4,512,512]{2,1,0:T(8,128)(2,1)} %param.16) | copy-start | bytes 6291460
Sparse Core Ops, SparseCore 0:
  9.1 77.2 all-gather.7
  88.0 44.1 all-gather.9
  139.4 23.5 reduce-scatter.3
